TPU v7x, 32 devices: a whole 2x2x4 slice. The times are simulated.
32 devices in a mesh: blk: 8 (over y, x, core), org: 4 (over z).
Axes of the slice: x: 2, y: 2, z: 4, core: 2. Of those that a mesh axis runs over, the one named last changes fastest.
Arguments:
- warm_labels: float32 [64, 512, 1024], P('blk', None, 'org'), may hold values from 0 to 6
- link_costs: float32 [4, 64, 512], P(None, 'blk'), may hold values from 0.05 to 1.5
- anchor_nodes: int32 [1024], P('org'), may hold values from 0 to 32767
- demand: float32 [1024], P('org'), may hold values from 0.2 to 2
Outputs:
- labels: float32 [64, 512, 1024], P('blk', None, 'org')
- link_weights: float32 [4, 64, 512], P(None, 'blk', 'org')
Inputs may be any that keep to these rules, and one draw needn't show every extreme that they name: `anchor_nodes`: node numbers r * 512 + c.
All inputs are finite; a program needn't handle non-finite values.
Results may differ from a plain program's by a relative error of at most 0.0003.
Values sent between devices are 32-bit elements; how exact they have to be, the bound alone decides.
A program may use at most 128 MiB of HBM per device.

v0:
```python
import jax
import jax.numpy as jnp
from jax import lax
from jax.sharding import PartitionSpec as P

ANCHORS = 1024
INNER = 2
ROUNDS = 3


far_value = 1000000000.0
temper = 0.5


def padded_2(cells, sides, width):
    for axis, dim in sides:
        count = lax.axis_size(axis)
        ends = count - 1
        head = lax.slice_in_dim(cells, 0, width, axis=dim)
        tail = lax.slice_in_dim(cells, cells.shape[dim] - width, cells.shape[dim], axis=dim)
        cells = jnp.concatenate(
            [
                lax.ppermute(tail, axis, [(i, (i + 1) % count) for i in range(ends)]),
                cells,
                lax.ppermute(head, axis, [((i + 1) % count, i) for i in range(ends)]),
            ],
            axis=dim,
        )
    return cells


def relax_step(padded, costs):
    centre = padded[1:-1]
    edge = jnp.full((centre.shape[0], 1, centre.shape[2]), far_value, centre.dtype)
    west = jnp.concatenate([edge, centre[:, :-1]], axis=1) + costs[0, 1:-1][:, :, None]
    east = jnp.concatenate([centre[:, 1:], edge], axis=1) + costs[1, 1:-1][:, :, None]
    north = padded[:-2] + costs[2, 1:-1][:, :, None]
    south = padded[2:] + costs[3, 1:-1][:, :, None]
    return jnp.minimum(jnp.minimum(jnp.minimum(centre, west), jnp.minimum(east, north)), south)


def link_terms(padded, labels, costs, weights):
    edge = jnp.full((labels.shape[0], 1, labels.shape[2]), far_value, labels.dtype)
    sides = (
        jnp.concatenate([edge, labels[:, :-1]], axis=1),
        jnp.concatenate([labels[:, 1:], edge], axis=1),
        padded[:-2],
        padded[2:],
    )
    result = []
    for side in range(4):
        expo = jnp.exp(-temper * (sides[side] + costs[side][:, :, None] - labels))
        result.append(jnp.einsum("rco,o->rc", expo, weights, precision=lax.Precision.HIGHEST))
    return jnp.stack(result)


def outside_far(padded, first_row, total_rows):
    global_row = first_row + jnp.arange(padded.shape[0], dtype=jnp.int32)
    inside = (global_row >= 0) & (global_row < total_rows)
    return jnp.where(inside[:, None, None], padded, far_value)


def local(warm_labels, link_costs, anchor_nodes, demand):
    row_count, col_count, anchor_count = warm_labels.shape
    total_rows = row_count * lax.axis_size("blk")
    first_row = lax.axis_index("blk") * row_count
    node_ids = (first_row + jnp.arange(row_count, dtype=jnp.int32))[
        :, None
    ] * col_count + jnp.arange(col_count, dtype=jnp.int32)[None, :]
    labels = jnp.where(
        node_ids[:, :, None] == anchor_nodes[None, None, :],
        jnp.zeros_like(warm_labels),
        warm_labels,
    )
    cost_pad = jnp.pad(link_costs, ((0, 0), (1, 1), (0, 0)))
    for sweep in range(ROUNDS * INNER):
        current = padded_2(labels, (("blk", 0),), 1)
        current = outside_far(current, first_row - 1, total_rows)
        labels = relax_step(current, cost_pad)
    padded = padded_2(labels, (("blk", 0),), 1)
    padded = outside_far(padded, first_row - 1, total_rows)
    partial_terms = link_terms(padded, labels, link_costs, demand) / ANCHORS
    link_weights = lax.psum_scatter(partial_terms, "org", scatter_dimension=2, tiled=True)
    return (labels, link_weights)


def solution(mesh):
    placed = (P("blk", None, "org"), P(None, "blk", None), P("org"), P("org"))
    return jax.shard_map(
        local,
        mesh=mesh,
        in_specs=placed,
        out_specs=(P("blk", None, "org"), P(None, "blk", "org")),
        check_vma=False,
    )
```

profile of v0, /device:TPU:4, one launch (start us, length us, event | category | flops | bytes accessed | tf_op | source)
XLA Modules:
  0.0 179.8 jit_solution(9866357946789970454)
XLA Ops:
  7.3 3.3 %compare_select_fusion = f32[8,512,256]{2,1,0:T(8,128)S(1)} fusion(f32[8,512,256]{2,1,0:T(8,128)} %param.4, s32[256]{0:T(256)} %param.6, s32[8,512]{1,0:T(8,128)S(1)} %iota_add_fusion), kind=kLoop, calls=%fused_computation.65 | loop fusion | flops 2097152 | bytes 8406016 | tf_op jit(solution)/shard_map/jit(_where)/select_n | solution.py:70
  14.7 4.5 %collective-permute-start.1 = (f32[1,512,256]{2,1,0:T(8,128)S(1)}, f32[1,512,256]{2,1,0:T(8,128)S(1)}, u32[]{:S(2)}, u32[]{:S(2)}) collective-permute-start(f32[1,512,256]{2,1,0:T(8,128)S(1)} %get-tuple-element.29), channel_id=1, source_target_pairs={{4,0},{8,4},{12,8},{16,12},{20,16},{24,20},{28,24},{5,1},{9,5},{13... | collective-permute-start | bytes 1572872 | tf_op jit(solution)/shard_map/ppermute | solution.py:25
  19.2 7.7 %collective-permute-done = f32[1,512,256]{2,1,0:T(8,128)S(1)} collective-permute-done((f32[1,512,256]{2,1,0:T(8,128)S(1)}, f32[1,512,256]{2,1,0:T(8,128)S(1)}, u32[]{:S(2)}, u32[]{:S(2)}) %collective-permute-start) | collective-permute-done | bytes 524320 | tf_op jit(solution)/shard_map/ppermute | solution.py:23
  31.4 2.9 %fusion.25 = f32[8,512,256]{2,1,0:T(8,128)S(1)} fusion(f32[10,512,256]{2,1,0:T(8,128)S(1)} %maximum_select_fusion, f32[8,511,256]{2,1,0:T(8,128)S(1)} %get-tuple-element.13, f32[8,511,256]{2,1,0:T(8,128)S(1)} %get-tuple-element.12, f32[8,512]{1,0:T(8,128)S(1)} %get-tuple-element.32, f32[8,512]{1,0:T(8,128)S(1)} %get-tuple-element.33, ...), kind=kLoop, calls=%fused_computation.48 | loop fusion | flops 8388608 | bytes 25214976 | tf_op jit(solution)/shard_map/min | solution.py:39
  36.4 4.7 %collective-permute-start.3 = (f32[1,512,256]{2,1,0:T(8,128)S(1)}, f32[1,512,256]{2,1,0:T(8,128)S(1)}, u32[]{:S(2)}, u32[]{:S(2)}) collective-permute-start(f32[1,512,256]{2,1,0:T(8,128)S(1)} %get-tuple-element.27), channel_id=1, source_target_pairs={{4,0},{8,4},{12,8},{16,12},{20,16},{24,20},{28,24},{5,1},{9,5},{13... | collective-permute-start | bytes 1572872 | tf_op jit(solution)/shard_map/ppermute | solution.py:25
  41.1 7.8 %collective-permute-done.2 = f32[1,512,256]{2,1,0:T(8,128)S(1)} collective-permute-done((f32[1,512,256]{2,1,0:T(8,128)S(1)}, f32[1,512,256]{2,1,0:T(8,128)S(1)}, u32[]{:S(2)}, u32[]{:S(2)}) %collective-permute-start.2) | collective-permute-done | bytes 524320 | tf_op jit(solution)/shard_map/ppermute | solution.py:23
  50.4 2.9 %fusion.22 = f32[8,512,256]{2,1,0:T(8,128)S(1)} fusion(f32[10,512,256]{2,1,0:T(8,128)S(1)} %maximum_select_fusion.1, f32[8,511,256]{2,1,0:T(8,128)S(1)} %get-tuple-element.11, f32[8,511,256]{2,1,0:T(8,128)S(1)} %get-tuple-element.10, f32[8,512]{1,0:T(8,128)S(1)} %get-tuple-element.32, f32[8,512]{1,0:T(8,128)S(1)} %get-tuple-element.33, ...), kind=kLoop, calls=%fused_computation.42 | loop fusion | flops 8388608 | bytes 25214976 | tf_op jit(solution)/shard_map/min | solution.py:39
  55.4 4.5 %collective-permute-start.5 = (f32[1,512,256]{2,1,0:T(8,128)S(1)}, f32[1,512,256]{2,1,0:T(8,128)S(1)}, u32[]{:S(2)}, u32[]{:S(2)}) collective-permute-start(f32[1,512,256]{2,1,0:T(8,128)S(1)} %get-tuple-element.25), channel_id=1, source_target_pairs={{4,0},{8,4},{12,8},{16,12},{20,16},{24,20},{28,24},{5,1},{9,5},{13... | collective-permute-start | bytes 1572872 | tf_op jit(solution)/shard_map/ppermute | solution.py:25
  59.9 6.8 %collective-permute-done.4 = f32[1,512,256]{2,1,0:T(8,128)S(1)} collective-permute-done((f32[1,512,256]{2,1,0:T(8,128)S(1)}, f32[1,512,256]{2,1,0:T(8,128)S(1)}, u32[]{:S(2)}, u32[]{:S(2)}) %collective-permute-start.4) | collective-permute-done | bytes 524320 | tf_op jit(solution)/shard_map/ppermute | solution.py:23
  68.2 2.9 %fusion.19 = f32[8,512,256]{2,1,0:T(8,128)S(1)} fusion(f32[10,512,256]{2,1,0:T(8,128)S(1)} %maximum_select_fusion.2, f32[8,511,256]{2,1,0:T(8,128)S(1)} %get-tuple-element.9, f32[8,511,256]{2,1,0:T(8,128)S(1)} %get-tuple-element.8, f32[8,512]{1,0:T(8,128)S(1)} %get-tuple-element.32, f32[8,512]{1,0:T(8,128)S(1)} %get-tuple-element.33, ...), kind=kLoop, calls=%fused_computation.36 | loop fusion | flops 8388608 | bytes 25214976 | tf_op jit(solution)/shard_map/min | solution.py:39
  73.1 4.6 %collective-permute-start.7 = (f32[1,512,256]{2,1,0:T(8,128)S(1)}, f32[1,512,256]{2,1,0:T(8,128)S(1)}, u32[]{:S(2)}, u32[]{:S(2)}) collective-permute-start(f32[1,512,256]{2,1,0:T(8,128)S(1)} %get-tuple-element.23), channel_id=1, source_target_pairs={{4,0},{8,4},{12,8},{16,12},{20,16},{24,20},{28,24},{5,1},{9,5},{13... | collective-permute-start | bytes 1572872 | tf_op jit(solution)/shard_map/ppermute | solution.py:25
  77.8 5.8 %collective-permute-done.6 = f32[1,512,256]{2,1,0:T(8,128)S(1)} collective-permute-done((f32[1,512,256]{2,1,0:T(8,128)S(1)}, f32[1,512,256]{2,1,0:T(8,128)S(1)}, u32[]{:S(2)}, u32[]{:S(2)}) %collective-permute-start.6) | collective-permute-done | bytes 524320 | tf_op jit(solution)/shard_map/ppermute | solution.py:23
  85.9 2.9 %fusion.16 = f32[8,512,256]{2,1,0:T(8,128)S(1)} fusion(f32[10,512,256]{2,1,0:T(8,128)S(1)} %maximum_select_fusion.3, f32[8,511,256]{2,1,0:T(8,128)S(1)} %get-tuple-element.7, f32[8,511,256]{2,1,0:T(8,128)S(1)} %get-tuple-element.6, f32[8,512]{1,0:T(8,128)S(1)} %get-tuple-element.32, f32[8,512]{1,0:T(8,128)S(1)} %get-tuple-element.33, ...), kind=kLoop, calls=%fused_computation.30 | loop fusion | flops 8388608 | bytes 25214976 | tf_op jit(solution)/shard_map/min | solution.py:39
  90.9 4.7 %collective-permute-start.9 = (f32[1,512,256]{2,1,0:T(8,128)S(1)}, f32[1,512,256]{2,1,0:T(8,128)S(1)}, u32[]{:S(2)}, u32[]{:S(2)}) collective-permute-start(f32[1,512,256]{2,1,0:T(8,128)S(1)} %get-tuple-element.21), channel_id=1, source_target_pairs={{4,0},{8,4},{12,8},{16,12},{20,16},{24,20},{28,24},{5,1},{9,5},{13... | collective-permute-start | bytes 1572872 | tf_op jit(solution)/shard_map/ppermute | solution.py:25
  95.6 5.8 %collective-permute-done.8 = f32[1,512,256]{2,1,0:T(8,128)S(1)} collective-permute-done((f32[1,512,256]{2,1,0:T(8,128)S(1)}, f32[1,512,256]{2,1,0:T(8,128)S(1)}, u32[]{:S(2)}, u32[]{:S(2)}) %collective-permute-start.8) | collective-permute-done | bytes 524320 | tf_op jit(solution)/shard_map/ppermute | solution.py:23
  103.8 2.9 %fusion.13 = f32[8,512,256]{2,1,0:T(8,128)S(1)} fusion(f32[10,512,256]{2,1,0:T(8,128)S(1)} %maximum_select_fusion.4, f32[8,511,256]{2,1,0:T(8,128)S(1)} %get-tuple-element.5, f32[8,511,256]{2,1,0:T(8,128)S(1)} %get-tuple-element.4, f32[8,512]{1,0:T(8,128)S(1)} %get-tuple-element.32, f32[8,512]{1,0:T(8,128)S(1)} %get-tuple-element.33, ...), kind=kLoop, calls=%fused_computation.24 | loop fusion | flops 8388608 | bytes 25214976 | tf_op jit(solution)/shard_map/min | solution.py:39
  108.8 4.7 %collective-permute-start.11 = (f32[1,512,256]{2,1,0:T(8,128)S(1)}, f32[1,512,256]{2,1,0:T(8,128)S(1)}, u32[]{:S(2)}, u32[]{:S(2)}) collective-permute-start(f32[1,512,256]{2,1,0:T(8,128)S(1)} %get-tuple-element.19), channel_id=1, source_target_pairs={{4,0},{8,4},{12,8},{16,12},{20,16},{24,20},{28,24},{5,1},{9,5},{13... | collective-permute-start | bytes 1572872 | tf_op jit(solution)/shard_map/ppermute | solution.py:25
  113.5 5.8 %collective-permute-done.10 = f32[1,512,256]{2,1,0:T(8,128)S(1)} collective-permute-done((f32[1,512,256]{2,1,0:T(8,128)S(1)}, f32[1,512,256]{2,1,0:T(8,128)S(1)}, u32[]{:S(2)}, u32[]{:S(2)}) %collective-permute-start.10) | collective-permute-done | bytes 524320 | tf_op jit(solution)/shard_map/ppermute | solution.py:23
  127.4 4.9 %collective-permute-start.13 = (f32[1,512,256]{2,1,0:T(8,128)S(1)}, f32[1,512,256]{2,1,0:T(8,128)S(1)}, u32[]{:S(2)}, u32[]{:S(2)}) collective-permute-start(f32[1,512,256]{2,1,0:T(8,128)S(1)} %get-tuple-element.17), channel_id=1, source_target_pairs={{4,0},{8,4},{12,8},{16,12},{20,16},{24,20},{28,24},{5,1},{9,5},{13... | collective-permute-start | bytes 1572872 | tf_op jit(solution)/shard_map/ppermute | solution.py:25
  132.3 4.7 %fusion.28 = f32[1,8,512]{2,0,1:T(1,128)S(1)} fusion(f32[256,1,1]{0,1,2:T(1,128)S(1)} %bitcast.21, f32[8,512,256]{2,1,0:T(8,128)S(1)} %fusion.10, f32[8,511,256]{2,1,0:T(8,128)S(1)} %get-tuple-element.15, f32[8,512]{1,0:T(8,128)S(1)} %get-tuple-element.31), kind=kOutput, calls=%fused_computation.53 | convolution fusion | flops 15728640 | bytes 8414208 | tf_op jit(solution)/shard_map/rco,o->rc/dot_general | solution.py:53
  137.0 4.8 %fusion.34 = f32[1,8,512]{2,0,1:T(1,128)S(1)} fusion(f32[256,1,1]{0,1,2:T(1,128)S(1)} %bitcast.20, f32[8,512,256]{2,1,0:T(8,128)S(1)} %fusion.10, f32[8,511,256]{2,1,0:T(8,128)S(1)} %get-tuple-element.14, f32[8,512]{1,0:T(8,128)S(1)} %get-tuple-element.30), kind=kOutput, calls=%fused_computation.59 | convolution fusion | flops 15728640 | bytes 8414208 | tf_op jit(solution)/shard_map/rco,o->rc/dot_general | solution.py:53
  142.5 4.5 %fusion.3 = f32[1,8,512]{2,0,1:T(1,128)S(1)} fusion(f32[256,1,1]{0,1,2:T(1,128)S(1)} %bitcast.23, f32[8,512,256]{2,1,0:T(8,128)S(1)} %fusion.10, f32[10,512,256]{2,1,0:T(8,128)S(1)} %maximum_select_fusion.6, f32[8,512]{1,0:T(8,128)S(1)} %get-tuple-element.32), kind=kOutput, calls=%fused_computation.11 | convolution fusion | flops 15728640 | bytes 8422400 | tf_op jit(solution)/shard_map/rco,o->rc/dot_general | solution.py:53
  147.1 4.5 %fusion.8 = f32[1,8,512]{2,0,1:T(1,128)S(1)} fusion(f32[256,1,1]{0,1,2:T(1,128)S(1)} %bitcast.22, f32[8,512,256]{2,1,0:T(8,128)S(1)} %fusion.10, f32[10,512,256]{2,1,0:T(8,128)S(1)} %maximum_select_fusion.6, f32[8,512]{1,0:T(8,128)S(1)} %get-tuple-element.33), kind=kOutput, calls=%fused_computation.16 | convolution fusion | flops 15728640 | bytes 8422400 | tf_op jit(solution)/shard_map/rco,o->rc/dot_general | solution.py:53
  152.2 20.8 %reduce-scatter.2.cloned.1.call-done = f32[4,8,128]{2,1,0:T(8,128)} async-done(((f32[4,8,512]{2,1,0:T(8,128)}), f32[4,8,128]{2,1,0:T(8,128)}) %reduce-scatter.2.cloned.1.call-update) | async-done | bytes 16400 | tf_op jit(solution)/shard_map/reduce_scatter | solution.py:83
  (56 shorter events, 35.6 us)
Async XLA Ops:
  7.2 125.2 %copy-start = (f32[256]{0:T(256)S(1)}, f32[256]{0:T(256)}, u32[]{:S(2)}) copy-start(f32[256]{0:T(256)} %param.7) | copy-start | bytes 3076
  7.2 165.8 %reduce-scatter.2.cloned.1.call-start = ((), (), s32[]{:S(2)}) async-start(), calls=%async_computation.1 | async-start | bytes 81920 | tf_op jit(solution)/shard_map/reduce_scatter | solution.py:83
  7.3 11.9 %copy-start.3 = (f32[4,8,512]{2,1,0:T(8,128)S(1)}, f32[4,8,512]{2,1,0:T(8,128)}, u32[]{:S(2)}) copy-start(f32[4,8,512]{2,1,0:T(8,128)} %param.5) | copy-start | bytes 196612
  10.6 2.0 %copy-start.2 = (f32[8,512,256]{2,1,0:T(8,128)}, f32[8,512,256]{2,1,0:T(8,128)S(1)}, u32[]{:S(2)}) copy-start(f32[8,512,256]{2,1,0:T(8,128)S(1)} %compare_select_fusion) | copy-start | bytes 12582916
  12.7 14.3 %collective-permute-start = (f32[1,512,256]{2,1,0:T(8,128)S(1)}, f32[1,512,256]{2,1,0:T(8,128)S(1)}, u32[]{:S(2)}, u32[]{:S(2)}) collective-permute-start(f32[1,512,256]{2,1,0:T(8,128)S(1)} %get-tuple-element.28), channel_id=1, source_target_pairs={{0,4},{4,8},{8,12},{12,16},{16,20},{20,24},{24,28},{1,5},{5,9},{9,... | collective-permute-start | bytes 1572872 | tf_op jit(solution)/shard_map/ppermute | solution.py:23
  14.7 13.2 %collective-permute-start.1 = (f32[1,512,256]{2,1,0:T(8,128)S(1)}, f32[1,512,256]{2,1,0:T(8,128)S(1)}, u32[]{:S(2)}, u32[]{:S(2)}) collective-permute-start(f32[1,512,256]{2,1,0:T(8,128)S(1)} %get-tuple-element.29), channel_id=1, source_target_pairs={{4,0},{8,4},{12,8},{16,12},{20,16},{24,20},{28,24},{5,1},{9,5},{13... | collective-permute-start | bytes 1572872 | tf_op jit(solution)/shard_map/ppermute | solution.py:25
  34.5 14.4 %collective-permute-start.2 = (f32[1,512,256]{2,1,0:T(8,128)S(1)}, f32[1,512,256]{2,1,0:T(8,128)S(1)}, u32[]{:S(2)}, u32[]{:S(2)}) collective-permute-start(f32[1,512,256]{2,1,0:T(8,128)S(1)} %get-tuple-element.26), channel_id=1, source_target_pairs={{0,4},{4,8},{8,12},{12,16},{16,20},{20,24},{24,28},{1,5},{5,9},{9,... | collective-permute-start | bytes 1572872 | tf_op jit(solution)/shard_map/ppermute | solution.py:23
  36.4 12.5 %collective-permute-start.3 = (f32[1,512,256]{2,1,0:T(8,128)S(1)}, f32[1,512,256]{2,1,0:T(8,128)S(1)}, u32[]{:S(2)}, u32[]{:S(2)}) collective-permute-start(f32[1,512,256]{2,1,0:T(8,128)S(1)} %get-tuple-element.27), channel_id=1, source_target_pairs={{4,0},{8,4},{12,8},{16,12},{20,16},{24,20},{28,24},{5,1},{9,5},{13... | collective-permute-start | bytes 1572872 | tf_op jit(solution)/shard_map/ppermute | solution.py:25
  53.4 13.2 %collective-permute-start.4 = (f32[1,512,256]{2,1,0:T(8,128)S(1)}, f32[1,512,256]{2,1,0:T(8,128)S(1)}, u32[]{:S(2)}, u32[]{:S(2)}) collective-permute-start(f32[1,512,256]{2,1,0:T(8,128)S(1)} %get-tuple-element.24), channel_id=1, source_target_pairs={{0,4},{4,8},{8,12},{12,16},{16,20},{20,24},{24,28},{1,5},{5,9},{9,... | collective-permute-start | bytes 1572872 | tf_op jit(solution)/shard_map/ppermute | solution.py:23
  55.4 11.3 %collective-permute-start.5 = (f32[1,512,256]{2,1,0:T(8,128)S(1)}, f32[1,512,256]{2,1,0:T(8,128)S(1)}, u32[]{:S(2)}, u32[]{:S(2)}) collective-permute-start(f32[1,512,256]{2,1,0:T(8,128)S(1)} %get-tuple-element.25), channel_id=1, source_target_pairs={{4,0},{8,4},{12,8},{16,12},{20,16},{24,20},{28,24},{5,1},{9,5},{13... | collective-permute-start | bytes 1572872 | tf_op jit(solution)/shard_map/ppermute | solution.py:25
  71.2 12.4 %collective-permute-start.6 = (f32[1,512,256]{2,1,0:T(8,128)S(1)}, f32[1,512,256]{2,1,0:T(8,128)S(1)}, u32[]{:S(2)}, u32[]{:S(2)}) collective-permute-start(f32[1,512,256]{2,1,0:T(8,128)S(1)} %get-tuple-element.22), channel_id=1, source_target_pairs={{0,4},{4,8},{8,12},{12,16},{16,20},{20,24},{24,28},{1,5},{5,9},{9,... | collective-permute-start | bytes 1572872 | tf_op jit(solution)/shard_map/ppermute | solution.py:23
  73.1 11.3 %collective-permute-start.7 = (f32[1,512,256]{2,1,0:T(8,128)S(1)}, f32[1,512,256]{2,1,0:T(8,128)S(1)}, u32[]{:S(2)}, u32[]{:S(2)}) collective-permute-start(f32[1,512,256]{2,1,0:T(8,128)S(1)} %get-tuple-element.23), channel_id=1, source_target_pairs={{4,0},{8,4},{12,8},{16,12},{20,16},{24,20},{28,24},{5,1},{9,5},{13... | collective-permute-start | bytes 1572872 | tf_op jit(solution)/shard_map/ppermute | solution.py:25
  89.0 12.5 %collective-permute-start.8 = (f32[1,512,256]{2,1,0:T(8,128)S(1)}, f32[1,512,256]{2,1,0:T(8,128)S(1)}, u32[]{:S(2)}, u32[]{:S(2)}) collective-permute-start(f32[1,512,256]{2,1,0:T(8,128)S(1)} %get-tuple-element.20), channel_id=1, source_target_pairs={{0,4},{4,8},{8,12},{12,16},{16,20},{20,24},{24,28},{1,5},{5,9},{9,... | collective-permute-start | bytes 1572872 | tf_op jit(solution)/shard_map/ppermute | solution.py:23
  90.9 11.4 %collective-permute-start.9 = (f32[1,512,256]{2,1,0:T(8,128)S(1)}, f32[1,512,256]{2,1,0:T(8,128)S(1)}, u32[]{:S(2)}, u32[]{:S(2)}) collective-permute-start(f32[1,512,256]{2,1,0:T(8,128)S(1)} %get-tuple-element.21), channel_id=1, source_target_pairs={{4,0},{8,4},{12,8},{16,12},{20,16},{24,20},{28,24},{5,1},{9,5},{13... | collective-permute-start | bytes 1572872 | tf_op jit(solution)/shard_map/ppermute | solution.py:25
  106.8 12.5 %collective-permute-start.10 = (f32[1,512,256]{2,1,0:T(8,128)S(1)}, f32[1,512,256]{2,1,0:T(8,128)S(1)}, u32[]{:S(2)}, u32[]{:S(2)}) collective-permute-start(f32[1,512,256]{2,1,0:T(8,128)S(1)} %get-tuple-element.18), channel_id=1, source_target_pairs={{0,4},{4,8},{8,12},{12,16},{16,20},{20,24},{24,28},{1,5},{5,9},{9,... | collective-permute-start | bytes 1572872 | tf_op jit(solution)/shard_map/ppermute | solution.py:23
  108.8 11.4 %collective-permute-start.11 = (f32[1,512,256]{2,1,0:T(8,128)S(1)}, f32[1,512,256]{2,1,0:T(8,128)S(1)}, u32[]{:S(2)}, u32[]{:S(2)}) collective-permute-start(f32[1,512,256]{2,1,0:T(8,128)S(1)} %get-tuple-element.19), channel_id=1, source_target_pairs={{4,0},{8,4},{12,8},{16,12},{20,16},{24,20},{28,24},{5,1},{9,5},{13... | collective-permute-start | bytes 1572872 | tf_op jit(solution)/shard_map/ppermute | solution.py:25
  124.6 22.5 %copy-start.1 = (f32[8,512,256]{2,1,0:T(8,128)}, f32[8,512,256]{2,1,0:T(8,128)S(1)}, u32[]{:S(2)}) copy-start(f32[8,512,256]{2,1,0:T(8,128)S(1)} %fusion.10) | copy-start | bytes 12582916
  125.5 16.3 %collective-permute-start.12 = (f32[1,512,256]{2,1,0:T(8,128)S(1)}, f32[1,512,256]{2,1,0:T(8,128)S(1)}, u32[]{:S(2)}, u32[]{:S(2)}) collective-permute-start(f32[1,512,256]{2,1,0:T(8,128)S(1)} %get-tuple-element.16), channel_id=1, source_target_pairs={{0,4},{4,8},{8,12},{12,16},{16,20},{20,24},{24,28},{1,5},{5,9},{9,... | collective-permute-start | bytes 1572872 | tf_op jit(solution)/shard_map/ppermute | solution.py:23
  127.4 14.4 %collective-permute-start.13 = (f32[1,512,256]{2,1,0:T(8,128)S(1)}, f32[1,512,256]{2,1,0:T(8,128)S(1)}, u32[]{:S(2)}, u32[]{:S(2)}) collective-permute-start(f32[1,512,256]{2,1,0:T(8,128)S(1)} %get-tuple-element.17), channel_id=1, source_target_pairs={{4,0},{8,4},{12,8},{16,12},{20,16},{24,20},{28,24},{5,1},{9,5},{13... | collective-permute-start | bytes 1572872 | tf_op jit(solution)/shard_map/ppermute | solution.py:25
Sparse Core Ops, SparseCore 0:
  152.4 20.6 reduce-scatter.1
where the time goes:
time: 182 us; the launch traced here: 180 us
  waiting for transfers between devices  64 us (35%)
  starting transfers between devices  46.2 us (25%)
  other arithmetic  28.5 us (16%)
  matrix products  18.5 us (10%)
  between operations  14.5 us (8%)
  local copies, waits for them, and re-layouts  8.16 us (4%)
    ppermute x7, waiting for transfers between devices, padded_2(): lax.ppermute(tail, axis, [(i, (i + 1) % count) for i in range(ends)])  39.8 us
    ppermute x7, starting transfers between devices, padded_2(): lax.ppermute(head, axis, [((i + 1) % count, i) for i in range(ends)])  32.7 us
    reduce_scatter x1, waiting for transfers between devices, local(): lax.psum_scatter(partial_terms, 'org', scatter_dimension=2, tiled=True)  20.8 us
    dot_general x4, matrix products, link_terms(): jnp.einsum('rco,o->rc', expo, weights, precision=lax.Precision.HIGHEST)  18.5 us
    min x6, other arithmetic, relax_step(): jnp.minimum(jnp.minimum(jnp.minimum(centre, west), jnp.minimum(east, nort...  17.6 us
    ppermute x7, starting transfers between devices, padded_2(): lax.ppermute(tail, axis, [(i, (i + 1) % count) for i in range(ends)])  13.4 us
    select_n x7, other arithmetic, outside_far(): return jnp.where(inside[:, None, None], padded, far_value)  6.88 us
    slice x6, local copies, waits for them, and re-layouts, relax_step(): centre[:, :-1]  4.81 us
  transfers between devices with their start and end apart: 15, of which 11 were waited for; matrix products, arithmetic and copies ran while one was open for 5% of the time, Pallas kernels for 0%

commit v1 on v0

v1 whole, which is shorter than its diff:
```python
import functools

import jax
import jax.numpy as jnp
from jax import lax
from jax.experimental import pallas as pl
from jax.experimental.pallas import tpu as pltpu
from jax.sharding import PartitionSpec as P

INNER = 2
ROUNDS = 3
STEPS = INNER * ROUNDS
HALO = STEPS + 1

far_value = 1000000000.0
temper = 0.5
LANES = 128
PAD = 8
CHUNK = 64
MESH = pl.DeviceIdType.MESH


def kernel(n, m, rows, cols, halves, warm, costs, anchors, demand, out, weights, grid, wide, raw, turned, sums, share,
           landed, row_send, row_recv, cost_send, cost_recv, org_send, org_recv, local_sem, out_sem):
    me = lax.axis_index("blk")
    org = lax.axis_index("org")
    has_top = me > 0
    has_bottom = me < n - 1
    top = {"blk": jnp.maximum(me - 1, 0)}
    bottom = {"blk": jnp.minimum(me + 1, n - 1)}
    first, last = HALO, HALO + rows - 1
    inner = pl.ds(PAD, cols)
    sides = ((has_top, top), (has_bottom, bottom))

    barrier = pltpu.get_barrier_semaphore()
    for there, who in sides:
        @pl.when(there)
        def _():
            pl.semaphore_signal(barrier, inc=1, device_id=who, device_id_type=MESH)
    for d in range(1, m):
        pl.semaphore_signal(barrier, inc=1, device_id={"org": lax.rem(org + d, m)}, device_id_type=MESH)
    own_cost = pltpu.make_async_copy(costs, raw.at[0], local_sem.at[halves])
    own_cost.start()

    def own_rows(h):
        return pltpu.make_async_copy(
            warm.at[:, :, pl.ds(h * LANES, LANES)],
            grid.at[0, h, pl.ds(first, rows), inner, :],
            local_sem.at[h])
    for h in range(halves):
        own_rows(h).start()
    pl.semaphore_wait(barrier, m - 1 + jnp.where(has_top, 1, 0) + jnp.where(has_bottom, 1, 0))

    def cost_copy(side):
        return pltpu.make_async_remote_copy(
            src_ref=costs, dst_ref=raw.at[2 - side], send_sem=cost_send.at[side], recv_sem=cost_recv.at[side],
            device_id=sides[side][1], device_id_type=MESH)

    def row_copy(side, h, j):
        source = j - 1 if side == 0 else rows - j
        target = last + j if side == 0 else first - j
        lanes = pl.ds(pl.multiple_of(h * LANES, LANES), LANES)
        return pltpu.make_async_remote_copy(
            src_ref=warm.at[source, :, lanes], dst_ref=grid.at[0, h, target, inner, :],
            send_sem=row_send.at[side, h, j - 1], recv_sem=row_recv.at[side, h, j - 1],
            device_id=sides[side][1], device_id_type=MESH)

    for side in range(2):
        @pl.when(sides[side][0])
        def _():
            cost_copy(side).start()
    for h in range(halves):
        def send_rows(j, carry):
            for side in range(2):
                @pl.when(sides[side][0])
                def _():
                    row_copy(side, h, j).start()
            return carry
        lax.fori_loop(1, HALO + 1, send_rows, 0)

    edge = jnp.full((PAD, LANES), far_value, jnp.float32)
    total = rows + 2 * HALO

    def fill_edges(r, carry):
        for b in range(2):
            for h in range(halves):
                grid[b, h, r, pl.ds(0, PAD), :] = edge
                grid[b, h, r, pl.ds(PAD + cols, PAD), :] = edge
        return carry
    lax.fori_loop(0, total, fill_edges, 0)
    raw[3] = jnp.zeros_like(raw[3])
    for missing, block, begin in ((me == 0, 1, 0), (me == n - 1, 2, last + 1)):
        @pl.when(missing)
        def _():
            raw[block] = jnp.full(raw.shape[1:], far_value, jnp.float32)
            def fill(r, carry):
                for h in range(halves):
                    grid[0, h, begin + r, inner, :] = jnp.full((cols, LANES), far_value, jnp.float32)
                return carry
            lax.fori_loop(0, HALO, fill, 0)

    own_cost.wait()
    for side in range(2):
        @pl.when(sides[1 - side][0])
        def _():
            cost_copy(side).wait_recv()
    turned[...] = jnp.transpose(raw[...].reshape(4 * 4 * rows, cols))

    def widen(i, carry):
        piece = turned[pl.ds(pl.multiple_of(i * 8, 8), 8), :]
        for r in range(1, total - 1):
            if r < first:
                block, row = 1, rows - first + r
            elif r <= last:
                block, row = 0, r - first
            else:
                block, row = 2, r - last - 1
            for k in range(4):
                lane = (block * 4 + k) * rows + row
                wide[k, r, pl.ds(pl.multiple_of(i * 8, 8), 8), :] = jnp.broadcast_to(piece[:, lane:lane + 1], (8, LANES))
        return carry
    lax.fori_loop(0, cols // 8, widen, 0)

    def place(h, r):
        names = anchors[h]
        base = (me * rows + r - first) * cols
        for i in range(cols // CHUNK):
            node = lax.broadcasted_iota(jnp.int32, (CHUNK, LANES), 0) + (base + i * CHUNK)
            at = pl.ds(PAD + i * CHUNK, CHUNK)
            grid[0, h, r, at, :] = jnp.where(node == names, 0.0, grid[0, h, r, at, :])

    def relax(h, r, s):
        old, new = lax.rem(s + 1, 2), lax.rem(s, 2)
        for i in range(cols // CHUNK):
            c0 = PAD + i * CHUNK
            at, cut = pl.ds(c0, CHUNK), pl.ds(i * CHUNK, CHUNK)
            best = grid[old, h, r, at, :]
            best = jnp.minimum(best, grid[old, h, r, pl.ds(c0 - 1, CHUNK), :] + wide[0, r, cut, :])
            best = jnp.minimum(best, grid[old, h, r, pl.ds(c0 + 1, CHUNK), :] + wide[1, r, cut, :])
            best = jnp.minimum(best, grid[old, h, r - 1, at, :] + wide[2, r, cut, :])
            best = jnp.minimum(best, grid[old, h, r + 1, at, :] + wide[3, r, cut, :])
            grid[new, h, r, at, :] = best

    ones = jnp.ones((8, 2 * LANES), jnp.bfloat16)
    sums[...] = jnp.zeros_like(sums)
    middle = rows // 2
    zero_edge = jnp.zeros((PAD, LANES), jnp.float32)

    def half(h, carry):
        own_rows(h).wait()

        def place_own(r, carry):
            place(h, r)
            return carry
        lax.fori_loop(first, last + 1, place_own, 0)
        for s in range(1, middle):
            def inside(r, carry):
                relax(h, r, jnp.int32(s))
                return carry
            lax.fori_loop(first + s, last - s + 1, inside, 0)

        def stage(j, carry):
            for side in range(2):
                @pl.when(sides[1 - side][0])
                def _():
                    row_copy(side, h, j).wait_recv()
            place(h, first - j)
            place(h, last + j)

            def diagonal(s, carry):
                relax(h, first - j + s, s)
                relax(h, last + j - s, s)
                return carry
            return lax.fori_loop(1, jnp.minimum(STEPS, j + middle - 1) + 1, diagonal, carry)
        lax.fori_loop(1, HALO + 1, stage, 0)
        out_copy(h).start()

        def small(r, carry):
            grid[1, h, r, pl.ds(0, PAD), :] = zero_edge
            grid[1, h, r, pl.ds(PAD + cols, PAD), :] = zero_edge
            for i in range(cols // CHUNK):
                at = pl.ds(PAD + i * CHUNK, CHUNK)
                grid[1, h, r, at, :] = jnp.exp(-temper * grid[0, h, r, at, :])
            return carry
        lax.fori_loop(first - 1, last + 2, small, 0)

        def add_links(q, carry):
            r = first + q
            own = demand[h] * jnp.exp(temper * grid[0, h, r, inner, :])
            places = ((r, PAD - 1), (r, PAD + 1), (r - 1, PAD), (r + 1, PAD))
            for k, (row, start) in enumerate(places):
                term = own * grid[1, h, row, pl.ds(start, cols), :]
                high = term.astype(jnp.bfloat16)
                low = (term - high.astype(jnp.float32)).astype(jnp.bfloat16)
                part = lax.dot_general(ones, jnp.concatenate([high, low], axis=1), (((1,), (1,)), ((), ())),
                                       preferred_element_type=jnp.float32)
                sums[k, pl.ds(q, 1), :] += part[0:1]
            return carry
        lax.fori_loop(0, rows, add_links, 0)
        return carry

    def out_copy(h):
        lanes = pl.ds(pl.multiple_of(h * LANES, LANES), LANES)
        return pltpu.make_async_copy(grid.at[0, h, pl.ds(first, rows), inner, :], out.at[:, :, lanes], out_sem.at[h])

    lax.fori_loop(0, halves, half, 0)

    scale = 1.0 / (m * halves * LANES)
    ours = sums[...] * jnp.exp(-temper * raw[0]) * scale
    width = cols // m
    for p in range(m):
        share[p] = ours[:, :, p * width:(p + 1) * width]

    def org_copy(d):
        peer = lax.rem(org + d, m)
        return pltpu.make_async_remote_copy(
            src_ref=share.at[peer], dst_ref=landed.at[d - 1], send_sem=org_send.at[d - 1], recv_sem=org_recv.at[d - 1],
            device_id={"org": peer}, device_id_type=MESH)
    for d in range(1, m):
        org_copy(d).start()
    final = share[org]
    for d in range(1, m):
        org_copy(d).wait_recv()
        final += landed[d - 1]
    weights[...] = final

    for d in range(1, m):
        org_copy(d).wait_send()
    for h in range(halves):
        out_copy(h).wait()
    for side in range(2):
        @pl.when(sides[side][0])
        def _():
            cost_copy(side).wait_send()
            for h in range(halves):
                def sent(j, carry):
                    row_copy(side, h, j).wait_send()
                    return carry
                lax.fori_loop(1, HALO + 1, sent, 0)


def local(n, m, warm_labels, link_costs, anchor_nodes, demand):
    rows, cols, count = warm_labels.shape
    halves = count // LANES
    total = rows + 2 * HALO
    width = cols // m
    any_space = pl.BlockSpec(memory_space=pl.ANY)
    vmem = pl.BlockSpec(memory_space=pltpu.VMEM)
    dma = pltpu.SemaphoreType.DMA
    return pl.pallas_call(
        functools.partial(kernel, n, m, rows, cols, halves),
        out_shape=(
            jax.ShapeDtypeStruct((rows, cols, count), jnp.float32),
            jax.ShapeDtypeStruct((4, rows, width), jnp.float32),
        ),
        in_specs=[any_space, any_space, vmem, vmem],
        out_specs=(any_space, vmem),
        scratch_shapes=[
            pltpu.VMEM((2, halves, total, cols + 2 * PAD, LANES), jnp.float32),
            pltpu.VMEM((4, total, cols, LANES), jnp.float32),
            pltpu.VMEM((4, 4, rows, cols), jnp.float32),
            pltpu.VMEM((cols, 16 * rows), jnp.float32),
            pltpu.VMEM((4, rows, cols), jnp.float32),
            pltpu.VMEM((m, 4, rows, width), jnp.float32),
            pltpu.VMEM((max(m - 1, 1), 4, rows, width), jnp.float32),
            dma((2, halves, HALO)),
            dma((2, halves, HALO)),
            dma((2,)),
            dma((2,)),
            dma((max(m - 1, 1),)),
            dma((max(m - 1, 1),)),
            dma((halves + 1,)),
            dma((halves,)),
        ],
        compiler_params=pltpu.CompilerParams(collective_id=0, has_side_effects=True, vmem_limit_bytes=60 * 1024 * 1024),
    )(warm_labels, link_costs, anchor_nodes.reshape(halves, 1, LANES), demand.reshape(halves, 1, LANES))


def solution(mesh):
    placed = (P("blk", None, "org"), P(None, "blk", None), P("org"), P("org"))
    return jax.shard_map(
        functools.partial(local, mesh.shape["blk"], mesh.shape["org"]),
        mesh=mesh,
        in_specs=placed,
        out_specs=(P("blk", None, "org"), P(None, "blk", "org")),
        check_vma=False,
    )
```

time: 182 us -> 102 us (0.56); the launches traced: 180 us -> 102 us
  Pallas kernels: 0 us -> 96.5 us
  waiting for transfers between devices: 64 us -> 0 us
  starting transfers between devices: 46.2 us -> 0 us
  other arithmetic: 28.5 us -> 0 us
  matrix products: 18.5 us -> 0 us
  between operations: 14.5 us -> 0.65 us
  local copies, waits for them, and re-layouts: 8.16 us -> 5.11 us
    pallas_call x0 -> x1, Pallas kernels: none -> 96.5 us  [local(): pl.pallas_call(functools.partial(kernel, n, m, rows, cols, halves), out_s...]
    ppermute x14 -> x0, starting transfers between devices: 46.2 us -> none  [the longest x7 32.7 us: padded_2(): lax.ppermute(head, axis, [((i + 1) % count, i) for i in range(ends)])]
    ppermute x14 -> x0, waiting for transfers between devices: 43.2 us -> none  [the longest x7 39.8 us: padded_2(): lax.ppermute(tail, axis, [(i, (i + 1) % count) for i in range(ends)])]
    reduce_scatter x1 -> x0, waiting for transfers between devices: 20.8 us -> none  [local(): lax.psum_scatter(partial_terms, 'org', scatter_dimension=2, tiled=True)]
    dot_general x4 -> x0, matrix products: 18.5 us -> none  [link_terms(): jnp.einsum('rco,o->rc', expo, weights, precision=lax.Precision.HIGHEST)]
    min x6 -> x0, other arithmetic: 17.6 us -> none  [relax_step(): jnp.minimum(jnp.minimum(jnp.minimum(centre, west), jnp.minimum(east, nort...]
    select_n x8 -> x0, other arithmetic: 10.2 us -> none  [the longest x7 6.88 us: outside_far(): return jnp.where(inside[:, None, None], padded, far_value)]
    slice x14 -> x0, local copies, waits for them, and re-layouts: 6.1 us -> none  [the longest x6 4.81 us: relax_step(): centre[:, :-1]]
  transfers between devices with their start and end apart: 15 -> 0, of which waited for: 11 -> 0; matrix products, arithmetic and copies ran while one was open for 5% -> 0% of each run, Pallas kernels for 0% -> 0%
where the time goes in v1:
time: 102 us
  Pallas kernels  96.5 us (95%)
  local copies, waits for them, and re-layouts  5.11 us (5%)
    pallas_call x1, Pallas kernels, local(): pl.pallas_call(functools.partial(kernel, n, m, rows, cols, halves), out_s...  96.5 us
    unnamed x4, local copies, waits for them, and re-layouts  5.11 us

profile of v1, /device:TPU:4, one launch (start us, length us, event | category | flops | bytes accessed | tf_op | source)
XLA Modules:
  0.0 102.2 jit_solution(3611647374270373597)
XLA Ops:
  0.6 96.5 %shard_map.59 = (f32[8,512,256]{2,1,0:T(8,128)}, f32[4,8,128]{2,1,0:T(8,128)}) custom-call(f32[8,512,256]{2,1,0:T(8,128)} %warm.1, f32[4,8,512]{2,1,0:T(8,128)} %costs.1, s32[2,1,128]{2,1,0:T(1,128)} %bitcast.2, f32[2,1,128]{2,1,0:T(1,128)} %bitcast.3), custom_call_target="tpu_custom_call" | custom-call | tf_op jit(solution)/shard_map/pallas_call | solution.py:250
  97.1 0.0 copy-start
  97.1 4.5 %copy.8 = f32[8,512,256]{2,1,0:T(8,128)} copy(f32[8,512,256]{2,1,0:T(8,128)} %get-tuple-element.4) | data formatting | bytes 8388608
  101.6 0.0 copy-done
  101.6 0.6 copy.9
Async XLA Ops:
  97.1 4.5 %copy-start = (f32[4,8,128]{2,1,0:T(8,128)S(1)}, f32[4,8,128]{2,1,0:T(8,128)}, u32[]{:S(2)}) copy-start(f32[4,8,128]{2,1,0:T(8,128)} %get-tuple-element.5) | copy-start | bytes 49156

commit v2 on v1

--- a/solution.py
+++ b/solution.py
@@ -18,10 +18,11 @@
 PAD = 8
 CHUNK = 64
 MESH = pl.DeviceIdType.MESH
+GROUPS = ((1, HALO - 3), (HALO - 2, HALO - 1), (HALO, HALO))
 
 
 def kernel(n, m, rows, cols, halves, warm, costs, anchors, demand, out, weights, grid, wide, raw, turned, sums, share,
-           landed, row_send, row_recv, cost_send, cost_recv, org_send, org_recv, local_sem, out_sem):
+           landed, relay, decay, row_send, row_recv, relay_in, relay_out, cost_send, cost_recv, org_send, org_recv, local_sem, out_sem):
     me = lax.axis_index("blk")
     org = lax.axis_index("org")
     has_top = me > 0
@@ -31,6 +32,12 @@
     first, last = HALO, HALO + rows - 1
     inner = pl.ds(PAD, cols)
     sides = ((has_top, top), (has_bottom, bottom))
+    mid = n // 2
+    relayed = n == 8
+    via = (0, n - 1)
+    goal = (mid - 1, mid)
+    splits = tuple(relayed and me == goal[1 - side] for side in range(2))
+    cut = cols // 2
 
     barrier = pltpu.get_barrier_semaphore()
     for there, who in sides:
@@ -39,6 +46,12 @@
             pl.semaphore_signal(barrier, inc=1, device_id=who, device_id_type=MESH)
     for d in range(1, m):
         pl.semaphore_signal(barrier, inc=1, device_id={"org": lax.rem(org + d, m)}, device_id_type=MESH)
+    if relayed:
+        for a, b in ((mid - 1, 0), (mid - 1, n - 1), (mid, 0), (mid, n - 1)):
+            for mine, other in ((a, b), (b, a)):
+                @pl.when(me == mine)
+                def _():
+                    pl.semaphore_signal(barrier, inc=1, device_id={"blk": other}, device_id_type=MESH)
     own_cost = pltpu.make_async_copy(costs, raw.at[0], local_sem.at[halves])
     own_cost.start()
 
@@ -49,34 +62,79 @@
             local_sem.at[h])
     for h in range(halves):
         own_rows(h).start()
-    pl.semaphore_wait(barrier, m - 1 + jnp.where(has_top, 1, 0) + jnp.where(has_bottom, 1, 0))
+    pl.semaphore_wait(barrier, m - 1 + jnp.where(has_top, 1, 0) + jnp.where(has_bottom, 1, 0)
+                      + (jnp.where((me == 0) | (me == n - 1) | (me == mid) | (me == mid - 1), 2, 0) if relayed else 0))
 
     def cost_copy(side):
         return pltpu.make_async_remote_copy(
             src_ref=costs, dst_ref=raw.at[2 - side], send_sem=cost_send.at[side], recv_sem=cost_recv.at[side],
             device_id=sides[side][1], device_id_type=MESH)
 
-    def row_copy(side, h, j):
-        source = j - 1 if side == 0 else rows - j
-        target = last + j if side == 0 else first - j
-        lanes = pl.ds(pl.multiple_of(h * LANES, LANES), LANES)
-        return pltpu.make_async_remote_copy(
-            src_ref=warm.at[source, :, lanes], dst_ref=grid.at[0, h, target, inner, :],
-            send_sem=row_send.at[side, h, j - 1], recv_sem=row_recv.at[side, h, j - 1],
+    def ranges(side, g):
+        low, high = GROUPS[g]
+        count = high - low + 1
+        if side == 0:
+            return pl.ds(low - 1, count), pl.ds(last + low, count), pl.ds(low - 1, count)
+        return pl.ds(rows - high, count), pl.ds(first - high, count), pl.ds(first - high, count)
+
+    def lane_range(h):
+        return pl.ds(pl.multiple_of(h * LANES, LANES), LANES)
+
+    def row_copy(side, h, g, width):
+        source, target, _ = ranges(side, g)
+        return pltpu.make_async_remote_copy(
+            src_ref=warm.at[source, pl.ds(0, width), lane_range(h)],
+            dst_ref=grid.at[0, h, target, pl.ds(PAD, width), :],
+            send_sem=row_send.at[side, h, g, 0], recv_sem=row_recv.at[side, h, g, 0],
             device_id=sides[side][1], device_id_type=MESH)
+
+    def to_relay(side, h, g):
+        source, _, slots = ranges(side, g)
+        return pltpu.make_async_remote_copy(
+            src_ref=warm.at[source, pl.ds(cut, cols - cut), lane_range(h)],
+            dst_ref=relay.at[h, slots],
+            send_sem=row_send.at[side, h, g, 1], recv_sem=relay_in.at[h, g],
+            device_id={"blk": via[side]}, device_id_type=MESH)
+
+    def from_relay(side, h, g):
+        _, target, slots = ranges(side, g)
+        return pltpu.make_async_remote_copy(
+            src_ref=relay.at[h, slots],
+            dst_ref=grid.at[0, h, target, pl.ds(PAD + cut, cols - cut), :],
+            send_sem=relay_out.at[h, g], recv_sem=row_recv.at[side, h, g, 1],
+            device_id={"blk": goal[side]}, device_id_type=MESH)
+
+    def each_send(h, g, act):
+        for side in range(2):
+            there, split = sides[side][0], splits[side]
+            @pl.when(there & jnp.logical_not(split) if relayed else there)
+            def _():
+                act(row_copy(side, h, g, cols))
+            if relayed:
+                @pl.when(split)
+                def _():
+                    act(to_relay(side, h, g))
+                    act(row_copy(side, h, g, cut))
+
+    def arrive(h, g):
+        for side in range(2):
+            there, split = sides[1 - side][0], splits[1 - side]
+            @pl.when(there & jnp.logical_not(split) if relayed else there)
+            def _():
+                row_copy(side, h, g, cols).wait_recv()
+            if relayed:
+                @pl.when(split)
+                def _():
+                    row_copy(side, h, g, cut).wait_recv()
+                    from_relay(side, h, g).wait_recv()
 
     for side in range(2):
         @pl.when(sides[side][0])
         def _():
             cost_copy(side).start()
     for h in range(halves):
-        def send_rows(j, carry):
-            for side in range(2):
-                @pl.when(sides[side][0])
-                def _():
-                    row_copy(side, h, j).start()
-            return carry
-        lax.fori_loop(1, HALO + 1, send_rows, 0)
+        for g in range(len(GROUPS)):
+            each_send(h, g, lambda copy: copy.start())
 
     edge = jnp.full((PAD, LANES), far_value, jnp.float32)
     total = rows + 2 * HALO
@@ -145,6 +203,9 @@
     sums[...] = jnp.zeros_like(sums)
     middle = rows // 2
     zero_edge = jnp.zeros((PAD, LANES), jnp.float32)
+    for r in range(rows + 2):
+        decay[r, pl.ds(0, PAD), :] = zero_edge
+        decay[r, pl.ds(PAD + cols, PAD), :] = zero_edge
 
     def half(h, carry):
         own_rows(h).wait()
@@ -160,10 +221,6 @@
             lax.fori_loop(first + s, last - s + 1, inside, 0)
 
         def stage(j, carry):
-            for side in range(2):
-                @pl.when(sides[1 - side][0])
-                def _():
-                    row_copy(side, h, j).wait_recv()
             place(h, first - j)
             place(h, last + j)
 
@@ -172,31 +229,55 @@
                 relax(h, last + j - s, s)
                 return carry
             return lax.fori_loop(1, jnp.minimum(STEPS, j + middle - 1) + 1, diagonal, carry)
-        lax.fori_loop(1, HALO + 1, stage, 0)
-        out_copy(h).start()
 
         def small(r, carry):
-            grid[1, h, r, pl.ds(0, PAD), :] = zero_edge
-            grid[1, h, r, pl.ds(PAD + cols, PAD), :] = zero_edge
             for i in range(cols // CHUNK):
                 at = pl.ds(PAD + i * CHUNK, CHUNK)
-                grid[1, h, r, at, :] = jnp.exp(-temper * grid[0, h, r, at, :])
+                decay[r - first + 1, at, :] = jnp.exp(-temper * grid[0, h, r, at, :])
             return carry
-        lax.fori_loop(first - 1, last + 2, small, 0)
-
-        def add_links(q, carry):
-            r = first + q
-            own = demand[h] * jnp.exp(temper * grid[0, h, r, inner, :])
-            places = ((r, PAD - 1), (r, PAD + 1), (r - 1, PAD), (r + 1, PAD))
-            for k, (row, start) in enumerate(places):
-                term = own * grid[1, h, row, pl.ds(start, cols), :]
-                high = term.astype(jnp.bfloat16)
-                low = (term - high.astype(jnp.float32)).astype(jnp.bfloat16)
-                part = lax.dot_general(ones, jnp.concatenate([high, low], axis=1), (((1,), (1,)), ((), ())),
-                                       preferred_element_type=jnp.float32)
-                sums[k, pl.ds(q, 1), :] += part[0:1]
+
+        def add_link(k, own, r, row, start):
+            term = own * decay[row - first + 1, pl.ds(start, cols), :]
+            high = term.astype(jnp.bfloat16)
+            low = (term - high.astype(jnp.float32)).astype(jnp.bfloat16)
+            part = lax.dot_general(ones, jnp.concatenate([high, low], axis=1), (((1,), (1,)), ((), ())),
+                                   preferred_element_type=jnp.float32)
+            sums[k, pl.ds(r - first, 1), :] += part[0:1]
+
+        def growth(r):
+            return demand[h] * jnp.exp(temper * grid[0, h, r, inner, :])
+
+        def along(r, carry):
+            own = growth(r)
+            add_link(0, own, r, r, PAD - 1)
+            add_link(1, own, r, r, PAD + 1)
             return carry
-        lax.fori_loop(0, rows, add_links, 0)
+
+        def across(r, carry):
+            add_link(3, growth(r), r, r + 1, PAD)
+            add_link(2, growth(r + 1), r + 1, r, PAD)
+            return carry
+
+        for g in range(len(GROUPS) - 1):
+            arrive(h, g)
+            lax.fori_loop(GROUPS[g][0], GROUPS[g][1] + 1, stage, 0)
+        out_copy(h).start()
+        lax.fori_loop(first, last + 1, small, 0)
+        lax.fori_loop(first, last + 1, along, 0)
+        lax.fori_loop(first, last, across, 0)
+        g = len(GROUPS) - 1
+        arrive(h, g)
+        lax.fori_loop(GROUPS[g][0], GROUPS[g][1] + 1, stage, 0)
+        for r, k, row in ((first, 2, first - 1), (last, 3, last + 1)):
+            small(row, 0)
+            add_link(k, growth(r), r, row, PAD)
+        if relayed:
+            for side in range(2):
+                @pl.when(me == via[side])
+                def _():
+                    for g in range(len(GROUPS)):
+                        to_relay(side, h, g).wait_recv()
+                        from_relay(side, h, g).start()
         return carry
 
     def out_copy(h):
@@ -232,11 +313,14 @@
         @pl.when(sides[side][0])
         def _():
             cost_copy(side).wait_send()
-            for h in range(halves):
-                def sent(j, carry):
-                    row_copy(side, h, j).wait_send()
-                    return carry
-                lax.fori_loop(1, HALO + 1, sent, 0)
+    for h in range(halves):
+        for g in range(len(GROUPS)):
+            each_send(h, g, lambda copy: copy.wait_send())
+            if relayed:
+                for side in range(2):
+                    @pl.when(me == via[side])
+                    def _():
+                        from_relay(side, h, g).wait_send()
 
 
 def local(n, m, warm_labels, link_costs, anchor_nodes, demand):
@@ -263,8 +347,12 @@
             pltpu.VMEM((4, rows, cols), jnp.float32),
             pltpu.VMEM((m, 4, rows, width), jnp.float32),
             pltpu.VMEM((max(m - 1, 1), 4, rows, width), jnp.float32),
-            dma((2, halves, HALO)),
-            dma((2, halves, HALO)),
+            pltpu.VMEM((halves, HALO, cols - cols // 2, LANES), jnp.float32),
+            pltpu.VMEM((rows + 2, cols + 2 * PAD, LANES), jnp.float32),
+            dma((2, halves, len(GROUPS), 2)),
+            dma((2, halves, len(GROUPS), 2)),
+            dma((halves, len(GROUPS))),
+            dma((halves, len(GROUPS))),
             dma((2,)),
             dma((2,)),
             dma((max(m - 1, 1),)),

time: 102 us -> 90.2 us (0.88)
  Pallas kernels: 96.5 us -> 84.3 us
    pallas_call x1, Pallas kernels: 96.5 us -> 84.3 us  [local(): pl.pallas_call(functools.partial(kernel, n, m, rows, cols, halves), out_s...]
where the time goes in v2:
time: 90.2 us; the launch traced here: 90.1 us
  Pallas kernels  84.3 us (93%)
  local copies, waits for them, and re-layouts  5.11 us (6%)
    pallas_call x1, Pallas kernels, local(): pl.pallas_call(functools.partial(kernel, n, m, rows, cols, halves), out_s...  84.3 us
    unnamed x4, local copies, waits for them, and re-layouts  5.11 us

profile of v2, /device:TPU:4, one launch (start us, length us, event | category | flops | bytes accessed | tf_op | source)
XLA Modules:
  0.0 90.1 jit_solution(4047321050880806169)
XLA Ops:
  0.6 84.3 %shard_map.59 = (f32[8,512,256]{2,1,0:T(8,128)}, f32[4,8,128]{2,1,0:T(8,128)}) custom-call(f32[8,512,256]{2,1,0:T(8,128)} %warm.1, f32[4,8,512]{2,1,0:T(8,128)} %costs.1, s32[2,1,128]{2,1,0:T(1,128)} %bitcast.2, f32[2,1,128]{2,1,0:T(1,128)} %bitcast.3), custom_call_target="tpu_custom_call" | custom-call | tf_op jit(solution)/shard_map/pallas_call | solution.py:334
  84.9 0.0 copy-start
  85.0 4.5 %copy.8 = f32[8,512,256]{2,1,0:T(8,128)} copy(f32[8,512,256]{2,1,0:T(8,128)} %get-tuple-element.4) | data formatting | bytes 8388608
  89.5 0.0 copy-done
  89.5 0.6 copy.9
Async XLA Ops:
  84.9 4.5 %copy-start = (f32[4,8,128]{2,1,0:T(8,128)S(1)}, f32[4,8,128]{2,1,0:T(8,128)}, u32[]{:S(2)}) copy-start(f32[4,8,128]{2,1,0:T(8,128)} %get-tuple-element.5) | copy-start | bytes 49156

commit v3 on v2

--- a/solution.py
+++ b/solution.py
@@ -207,7 +207,7 @@
         decay[r, pl.ds(0, PAD), :] = zero_edge
         decay[r, pl.ds(PAD + cols, PAD), :] = zero_edge
 
-    def half(h, carry):
+    def begin(h, carry):
         own_rows(h).wait()
 
         def place_own(r, carry):
@@ -219,6 +219,17 @@
                 relax(h, r, jnp.int32(s))
                 return carry
             lax.fori_loop(first + s, last - s + 1, inside, 0)
+        return carry
+    lax.fori_loop(0, halves, begin, 0)
+
+    def half(h, carry):
+        if relayed:
+            for side in range(2):
+                @pl.when(me == via[side])
+                def _():
+                    for g in range(len(GROUPS)):
+                        to_relay(side, h, g).wait_recv()
+                        from_relay(side, h, g).start()
 
         def stage(j, carry):
             place(h, first - j)
@@ -271,13 +282,6 @@
         for r, k, row in ((first, 2, first - 1), (last, 3, last + 1)):
             small(row, 0)
             add_link(k, growth(r), r, row, PAD)
-        if relayed:
-            for side in range(2):
-                @pl.when(me == via[side])
-                def _():
-                    for g in range(len(GROUPS)):
-                        to_relay(side, h, g).wait_recv()
-                        from_relay(side, h, g).start()
         return carry
 
     def out_copy(h):

time: 90.2 us -> 83.8 us (0.929)
  the two profiles are of different devices: /device:TPU:4 before, /device:TPU:1 now
where the time goes in v3:
time: 83.8 us; the launch traced here: 83.7 us
  Pallas kernels  77.9 us (93%)
  local copies, waits for them, and re-layouts  5.11 us (6%)
    pallas_call x1, Pallas kernels, local(): pl.pallas_call(functools.partial(kernel, n, m, rows, cols, halves), out_s...  77.9 us
    unnamed x4, local copies, waits for them, and re-layouts  5.11 us

profile of v3, /device:TPU:1, one launch (start us, length us, event | category | flops | bytes accessed | tf_op | source)
XLA Modules:
  0.0 83.7 jit_solution(3159955196474723322)
XLA Ops:
  0.6 77.9 %shard_map.59 = (f32[8,512,256]{2,1,0:T(8,128)}, f32[4,8,128]{2,1,0:T(8,128)}) custom-call(f32[8,512,256]{2,1,0:T(8,128)} %warm.1, f32[4,8,512]{2,1,0:T(8,128)} %costs.1, s32[2,1,128]{2,1,0:T(1,128)} %bitcast.2, f32[2,1,128]{2,1,0:T(1,128)} %bitcast.3), custom_call_target="tpu_custom_call" | custom-call | tf_op jit(solution)/shard_map/pallas_call | solution.py:338
  78.5 0.0 copy-start
  78.6 4.5 %copy.8 = f32[8,512,256]{2,1,0:T(8,128)} copy(f32[8,512,256]{2,1,0:T(8,128)} %get-tuple-element.4) | data formatting | bytes 8388608
  83.1 0.0 copy-done
  83.1 0.6 copy.9
Async XLA Ops:
  78.5 4.5 %copy-start = (f32[4,8,128]{2,1,0:T(8,128)S(1)}, f32[4,8,128]{2,1,0:T(8,128)}, u32[]{:S(2)}) copy-start(f32[4,8,128]{2,1,0:T(8,128)} %get-tuple-element.5) | copy-start | bytes 49156
